TPU v7x, 512 devices: a whole 4x4x16 slice. The times are simulated.
512 devices in a mesh: param: 64 (over x_hi, z, core), qoi: 8 (over x_lo, y).
Axes of the slice: x: 4 (x_hi: 2, x_lo: 2; x = x_hi * 2 + x_lo), y: 4, z: 16, core: 2. Of those that a mesh axis runs over, the one named last changes fastest.
Arguments:
- samples: bfloat16 [64, 20480, 420], P('qoi', 'param'), may hold values from -16 to 16
- operator_rows: bfloat16 [8, 20480, 2, 2048], P(None, 'param', None, 'qoi'), may hold values from -0.03125 to 0.03125
- block_start: int32 [1], replicated, may hold values from 0 to 203
- gauge_group: int32 [2048], P('qoi'), may hold values from 0 to 15
Outputs:
- qoi_spectrum: float32 [64, 2, 8, 2048], P('param', None, None, 'qoi')
- segment_response: float32 [64, 2, 8, 16], P('param')
Inputs may be any that keep to these rules, and one draw needn't show every extreme that they name: `block_start`: the block's frequencies lie among the 211 frequencies of a real transform.
All inputs are finite; a program needn't handle non-finite values.
Results may differ from a plain program's by a relative error of at most 0.005.
Values may be sent and summed in bfloat16 or wider, within the bound.
A program may use at most 64 MiB of HBM per device.

v0:
```python
import math

import jax
import jax.numpy as jnp
from jax import lax
from jax.sharding import PartitionSpec as P

GROUPS = 16


def joined_along(pieces, dim):
    dims = list(pieces.shape[1:])
    dims[dim] *= pieces.shape[0]
    return jnp.moveaxis(pieces, 0, dim).reshape(dims)


def sent_to_all(value, axis):
    size = lax.axis_size(axis)
    return lax.all_to_all(
        jnp.broadcast_to(value[None], (size, *value.shape)), axis, 0, 0, tiled=True
    )


def gathered_copies(value, axis, dim):
    return joined_along(sent_to_all(value, axis), dim)


def over_copies(value, axis):
    everything = sent_to_all(value, axis)
    return jnp.sum(everything, axis=0)


def build_table(block_start, steps_count, freq_count):
    time_index = jnp.arange(steps_count, dtype=jnp.int32)
    freq_index = block_start[0] + jnp.arange(freq_count, dtype=jnp.int32)
    phase_index = time_index[:, None] * freq_index[None, :] % steps_count
    phases = phase_index.astype(jnp.float32) * (2.0 * math.pi / steps_count)
    table = jnp.concatenate([jnp.cos(phases), -jnp.sin(phases)], axis=1) / math.sqrt(steps_count)
    table_high = lax.optimization_barrier(table.astype(jnp.bfloat16))
    table_low = (table - table_high.astype(jnp.float32)).astype(jnp.bfloat16)
    return jnp.concatenate([table_high, table_low], axis=1)


def transform(series, combined, freq_count):
    sample_count, param_local, steps_count = series.shape
    flat = series.reshape(sample_count * param_local, steps_count)
    halves = jnp.dot(flat, combined, preferred_element_type=jnp.float32)
    spectrum = (halves[:, : 2 * freq_count] + halves[:, 2 * freq_count :]).astype(jnp.bfloat16)
    return spectrum.reshape(sample_count, param_local, 2, freq_count).transpose(3, 2, 0, 1)


def local(samples, operator_rows, block_start, gauge_group):
    freq_count = operator_rows.shape[0]
    param_local = operator_rows.shape[1]
    gauge_local = operator_rows.shape[3]
    combined = build_table(block_start, samples.shape[2], freq_count)
    spectra = gathered_copies(transform(samples, combined, freq_count), "qoi", 2)
    sample_total = spectra.shape[2]
    weights = operator_rows.reshape(freq_count, param_local, 2 * gauge_local)
    param_count = lax.axis_size("param")
    own_rows = sample_total // param_count
    product = jnp.einsum("fkcp,fpx->ckfx", spectra, weights, preferred_element_type=jnp.float32)
    real_part = product[:, 0, :, :gauge_local] - product[:, 1, :, gauge_local:]
    imag_part = product[:, 0, :, gauge_local:] + product[:, 1, :, :gauge_local]
    all_terms = jnp.stack([real_part, imag_part], axis=1)
    received = lax.all_to_all(
        all_terms.astype(jnp.bfloat16), "param", split_axis=0, concat_axis=0, tiled=True
    ).astype(all_terms.dtype)
    qoi_spectrum = jnp.sum(
        received.reshape(param_count, own_rows, 2, freq_count, gauge_local), axis=0
    )
    onehot = (gauge_group[:, None] == jnp.arange(GROUPS, dtype=jnp.int32)[None, :]).astype(
        jnp.float32
    )
    local_sums = jnp.dot(
        qoi_spectrum.reshape(-1, gauge_local),
        onehot,
        precision=lax.Precision.HIGHEST,
        preferred_element_type=jnp.float32,
    )
    local_sums = local_sums.reshape(own_rows, 2, freq_count, GROUPS)
    summed = over_copies(local_sums, "qoi")
    norm_factor = math.sqrt(GROUPS / (gauge_local * lax.axis_size("qoi")))
    return (qoi_spectrum, summed * norm_factor)


def solution(mesh):
    return jax.shard_map(
        local,
        mesh=mesh,
        in_specs=(P("qoi", "param", None), P(None, "param", None, "qoi"), P(), P("qoi")),
        out_specs=(P("param", None, None, "qoi"), P("param", None, None, None)),
        check_vma=False,
    )
```

profile of v0, /device:TPU:1, one launch (start us, length us, event | category | flops | bytes accessed | tf_op | source)
XLA Modules:
  0.0 89.6 jit_solution(12203857067298681651)
XLA Ops:
  1.3 0.2 fusion.18
  1.5 4.1 %reshape.45 = bf16[2560,420]{0,1:T(8,128)(2,1)S(1)} reshape(bf16[8,320,420]{1,0,2:T(8,128)(2,1)} %param.4) | data formatting | bytes 4300800 | tf_op jit(solution)/shard_map/reshape | solution.py:46
  5.6 0.5 convolution_bitcast_fusion
  6.1 0.1 reshape.46
  6.2 0.9 %broadcast_in_dim.4 = bf16[8,8,2,8,320]{4,3,2,1,0:T(8,128)(2,1)} broadcast(bf16[8,2,8,320]{3,2,1,0:T(8,128)(2,1)S(1)} %copy.19), dimensions={1,2,3,4} | broadcast | bytes 737280 | tf_op jit(solution)/shard_map/broadcast_in_dim | solution.py:20
  7.2 5.9 %all-to-all-start = ((bf16[8,8,2,8,320]{4,3,2,1,0:T(8,128)(2,1)}), bf16[8,8,2,8,320]{4,3,2,1,0:T(8,128)(2,1)S(1)}, u32[]{:S(2)}, u32[]{:S(2)}) async-start(bf16[8,8,2,8,320]{4,3,2,1,0:T(8,128)(2,1)} %broadcast_in_dim.4), calls=%async_computation | async-start | bytes 1572864 | tf_op jit(solution)/shard_map/all_to_all | solution.py:19
  13.1 4.2 %reshape.49 = bf16[8,320,512,1]{2,1,0,3:T(8,128)(2,1)S(1)} reshape(bf16[8,320,2,256]{3,2,1,0:T(2,128)(2,1)} %param.5) | data formatting | bytes 5242880 | tf_op jit(solution)/shard_map/reshape | solution.py:59
  17.3 4.2 %all-to-all-done = bf16[8,8,2,8,320]{4,3,2,1,0:T(8,128)(2,1)S(1)} async-done(((bf16[8,8,2,8,320]{4,3,2,1,0:T(8,128)(2,1)}), bf16[8,8,2,8,320]{4,3,2,1,0:T(8,128)(2,1)S(1)}, u32[]{:S(2)}, u32[]{:S(2)}) %all-to-all-start) | async-done | bytes 655392 | tf_op jit(solution)/shard_map/all_to_all | solution.py:19
  21.5 0.7 fusion.2
  22.2 0.1 fusion.8
  22.3 0.0 copy-start
  22.3 0.1 pad_maximum_fusion
  22.4 0.5 copy.21
  22.9 55.5 %all_to_all.15 = bf16[64,2,8,256]{3,1,2,0:T(2,128)(2,1)S(1)} all-to-all(bf16[64,2,8,256]{3,1,2,0:T(2,128)(2,1)S(1)} %copy.21), channel_id=1, replica_groups=mesh['param'=64,'qoi'=8] {'param'}, dimensions={0} | all-to-all | bytes 1048576 | tf_op jit(solution)/shard_map/all_to_all | solution.py:66
  78.5 0.1 convert_reduce_fusion
  78.5 0.0 copy-done
  78.5 0.1 fusion.21
  78.7 0.7 reshape.52
  79.4 3.3 %all-to-all-start.2 = ((f32[8,1,256]{2,1,0:T(1,128)}), f32[8,1,256]{2,1,0:T(1,128)S(1)}, u32[]{:S(2)}, u32[]{:S(2)}) async-start(f32[8,1,256]{2,1,0:T(1,128)} %reshape.52), calls=%async_computation.2 | async-start | bytes 16384 | tf_op jit(solution)/shard_map/all_to_all | solution.py:19
  82.7 0.6 copy.25
  83.4 4.3 %all-to-all-done.2 = f32[8,1,256]{2,1,0:T(1,128)S(1)} async-done(((f32[8,1,256]{2,1,0:T(1,128)}), f32[8,1,256]{2,1,0:T(1,128)S(1)}, u32[]{:S(2)}, u32[]{:S(2)}) %all-to-all-start.2) | async-done | bytes 8224 | tf_op jit(solution)/shard_map/all_to_all | solution.py:19
  87.7 0.5 broadcast.21
  88.2 0.7 reduce.3
  88.9 0.1 reshape.53
  89.0 0.6 multiply_bitcast_fusion
  (8 shorter events, 0.1 us)
Async XLA Ops:
  7.2 14.3 %all-to-all-start = ((bf16[8,8,2,8,320]{4,3,2,1,0:T(8,128)(2,1)}), bf16[8,8,2,8,320]{4,3,2,1,0:T(8,128)(2,1)S(1)}, u32[]{:S(2)}, u32[]{:S(2)}) async-start(bf16[8,8,2,8,320]{4,3,2,1,0:T(8,128)(2,1)} %broadcast_in_dim.4), calls=%async_computation | async-start | bytes 1572864 | tf_op jit(solution)/shard_map/all_to_all | solution.py:19
  22.3 56.2 %copy-start = (s32[256]{0:T(256)S(1)}, s32[256]{0:T(256)}, u32[]{:S(2)}) copy-start(s32[256]{0:T(256)} %param.7) | copy-start | bytes 3076
  79.4 8.3 %all-to-all-start.2 = ((f32[8,1,256]{2,1,0:T(1,128)}), f32[8,1,256]{2,1,0:T(1,128)S(1)}, u32[]{:S(2)}, u32[]{:S(2)}) async-start(f32[8,1,256]{2,1,0:T(1,128)} %reshape.52), calls=%async_computation.2 | async-start | bytes 16384 | tf_op jit(solution)/shard_map/all_to_all | solution.py:19
where the time goes:
time: 90 us; the launch traced here: 89.6 us
  blocking collectives  55.5 us (62%)
  local copies, waits for them, and re-layouts  11.8 us (13%)
  starting transfers between devices  9.27 us (10%)
  waiting for transfers between devices  8.52 us (9%)
  other arithmetic  1.73 us (2%)
  between operations  1.42 us (2%)
  matrix products  1.31 us (1%)
    all_to_all x1, blocking collectives, local(): lax.all_to_all(all_terms.astype(jnp.bfloat16), 'param', split_axis=0, con...  55.5 us
    all_to_all x2, starting transfers between devices, sent_to_all(): lax.all_to_all(jnp.broadcast_to(value[None], (size, *value.shape)), axis,...  9.27 us
    all_to_all x2, waiting for transfers between devices, sent_to_all(): lax.all_to_all(jnp.broadcast_to(value[None], (size, *value.shape)), axis,...  8.52 us
    reshape x1, local copies, waits for them, and re-layouts, local(): weights = operator_rows.reshape(freq_count, param_local, 2 * gauge_local)  4.15 us
    reshape x1, local copies, waits for them, and re-layouts, transform(): flat = series.reshape(sample_count * param_local, steps_count)  4.09 us
  transfers between devices with their start and end apart: 2, of which 2 were waited for; matrix products, arithmetic and copies ran while one was open for 5% of the time, Pallas kernels for 0%

commit v1 on v0

v1 whole, which is shorter than its diff:
```python
import functools
import math

import jax
import jax.numpy as jnp
from jax import lax
from jax.experimental import pallas as pl
from jax.experimental.pallas import tpu as pltpu
from jax.sharding import PartitionSpec as P

GROUPS = 16
MESH = pl.DeviceIdType.MESH
BF = jnp.bfloat16
F32 = jnp.float32

NQ = 8
NX = 2
NZ = 16
NF = 8
NT = 420
NS = 8
NP = 320
NG = 256
LANES = 2 * NP
STEPS = ((0, 100), (100, 128), (228, 96), (324, 96))
NEAR = 4


def owner_offsets():
    pairs = [(dx, dz) for dx in range(NX) for dz in range(-NZ // 2 + 1, NZ // 2 + 1) if (dx, dz) != (0, 0)]
    return sorted(pairs, key=lambda pair: (-(abs(pair[1]) + 2 * pair[0]), -pair[1]))


def phase_rows(first, begin, width):
    lane = lax.broadcasted_iota(jnp.int32, (NF, width), 1) + begin
    freq = lax.broadcasted_iota(jnp.int32, (NF, width), 0) + first
    turns = ((lane >> 3) * freq).astype(F32)
    rest = turns - NT * jnp.floor(turns * (1.0 / NT))
    quarter = jnp.floor(rest * (4.0 / NT) + 0.5)
    angle = (rest - (NT // 4) * quarter) * (2.0 * math.pi / NT)
    sq = angle * angle
    sine = angle * (1.0 + sq * (-1.0 / 6 + sq * (1.0 / 120 + sq * (-1.0 / 5040 + sq * (1.0 / 362880)))))
    cosine = 1.0 + sq * (-0.5 + sq * (1.0 / 24 + sq * (-1.0 / 720 + sq * (1.0 / 40320 + sq * (-1.0 / 3628800)))))
    odd = (quarter == 1.0) | (quarter == 3.0)
    scale = 1.0 / math.sqrt(NT)
    cos_all = jnp.where(odd, sine, cosine) * jnp.where((quarter == 1.0) | (quarter == 2.0), -scale, scale)
    sin_all = jnp.where(odd, cosine, sine) * jnp.where((quarter == 2.0) | (quarter == 3.0), scale, -scale)
    return cos_all, sin_all


def fill_table(first, core, rows_ref, table_ref):
    full = NT * NS
    for begin in range(0, full, 512):
        width = min(512, full - begin)
        rows_ref[0, :, begin : begin + width], rows_ref[1, :, begin : begin + width] = phase_rows(first, begin, width)
    for begin in range(0, full, 512):
        width = min(512, full - begin)
        span = slice(begin, begin + width)
        sample = lax.broadcasted_iota(jnp.int32, (16, width), 1) % NS
        row = lax.broadcasted_iota(jnp.int32, (16, width), 0)
        member = row // 8
        side = jnp.where(member == 0, core, 1 - core)
        hit = sample == (row % 4) * 2 + side
        upper = (row % 8) // 4 == 1
        for part in range(2):
            for pair in range(NF // 2):
                low = jnp.broadcast_to(rows_ref[part, 2 * pair : 2 * pair + 1, span], (16, width))
                high = jnp.broadcast_to(rows_ref[part, 2 * pair + 1 : 2 * pair + 2, span], (16, width))
                value = jnp.where(hit, jnp.where(upper, high, low), 0.0)
                rounded = value.astype(BF)
                at = part * 64 + pair * 16
                table_ref[at : at + 16, span] = rounded
                table_ref[128 + at : 144 + at, span] = (value - rounded.astype(F32)).astype(BF)


def planar(f, w_ref, order_ref, out_ref):
    for begin in range(0, NP, 128):
        count = min(128, NP - begin)
        rows = w_ref[f, begin : begin + count].reshape(2 * count, NG)
        order = order_ref[0] if count == 128 else order_ref[1, : 2 * count, : 2 * count]
        out_ref[f, 2 * begin : 2 * (begin + count)] = jnp.dot(order, rows, preferred_element_type=F32).astype(BF)


def kernel(
    x_hbm, w_hbm, first_hbm, group_hbm, acc_out, seg_out,
    x_v, table, rows, w_v, w_p, order, spectra, give, take, own, spread, send, recv, segs, first_s, group_v,
    x_sem, w_sem, first_sem, group_sem, ag_send, ag_recv, core_send, core_recv, rs_send, rs_recv, seg_send, seg_recv,
    far, line,
):
    pi, qj = lax.axis_index("param"), lax.axis_index("qoi")
    core, chip = pi % 2, pi // 2
    xh, z = chip // NZ, chip % NZ

    def param_at(dx, dz, dc=0):
        return (((xh + dx) % NX) * NZ + (z + dz + NZ) % NZ) * 2 + (core + dc) % 2

    first_copy = pltpu.make_async_copy(first_hbm, first_s, first_sem)
    first_copy.start()
    x_copies = [
        pltpu.make_async_copy(x_hbm.at[pl.ds(t0, n)], x_v.at[pl.ds(t0, n)], x_sem.at[i]) for i, (t0, n) in enumerate(STEPS)
    ]
    for copy in x_copies:
        copy.start()
    w_copy = pltpu.make_async_copy(w_hbm, w_v, w_sem)
    w_copy.start()
    group_copy = pltpu.make_async_copy(group_hbm, group_v, group_sem)
    group_copy.start()

    barrier = pltpu.get_barrier_semaphore()
    near = [(param_at(0, dz), qj) for dz in range(-NEAR, NEAR + 1) if dz]
    near += [(param_at(1, 0), qj), (param_at(0, 0, 1), qj)]
    near += [(pi, (qj + d) % NQ) for d in range(1, NQ)]
    for peer in near:
        pl.semaphore_signal(barrier, inc=1, device_id=peer, device_id_type=MESH)

    big = lax.broadcasted_iota(jnp.int32, (256, 256), 0)
    col = lax.broadcasted_iota(jnp.int32, (256, 256), 1)
    order[0] = jnp.where(col == (big % 128) * 2 + big // 128, 1.0, 0.0).astype(BF)
    order[1] = jnp.where(col == (big % 64) * 2 + (big // 64) % 2, 1.0, 0.0).astype(BF)

    first_copy.wait()
    fill_table(first_s[0], core, rows, table)

    halves = jnp.zeros((256, NP), F32)
    for copy, (t0, n) in zip(x_copies, STEPS):
        copy.wait()
        steps = x_v[t0 : t0 + n].reshape(n * NS, NP)
        halves += jnp.dot(table[:, t0 * NS : (t0 + n) * NS], steps, preferred_element_type=F32)
    spectrum = (halves[:128] + halves[128:]).astype(BF)
    real, imag = spectrum[:64], spectrum[64:]
    for block in range(2):
        spectra[qj, :, 256 * block : 256 * block + 128] = real[:, 128 * block : 128 * block + 128]
        spectra[qj, :, 256 * block + 128 : 256 * block + 256] = imag[:, 128 * block : 128 * block + 128]
    spectra[qj, :, 512:640] = jnp.concatenate([real[:, 256:320], imag[:, 256:320]], axis=1)

    pl.semaphore_wait(barrier, len(near))
    ag = [
        pltpu.make_async_remote_copy(
            src_ref=spectra.at[qj], dst_ref=spectra.at[qj], send_sem=ag_send.at[d - 1], recv_sem=ag_recv.at[d - 1],
            device_id=(pi, (qj + d) % NQ), device_id_type=MESH,
        )
        for d in range(1, NQ)
    ]
    for copy in ag:
        copy.start()
    for dz in (-NEAR, NEAR):
        pl.semaphore_signal(far, inc=1, device_id=(param_at(0, dz), qj), device_id_type=MESH)

    w_copy.wait()

    def planar_step(f, carry):
        planar(f, w_v, order, w_p)
        return carry

    lax.fori_loop(0, NF // 2, planar_step, 0)
    pl.semaphore_wait(far, 2)
    pl.semaphore_signal(line, inc=1, device_id=(param_at(1, 0), qj), device_id_type=MESH)
    lax.fori_loop(NF // 2, NF, planar_step, 0)
    for copy in ag:
        copy.wait()

    core_copies = []
    even = (lax.broadcasted_iota(jnp.int32, (256, NG), 0) % 8) < 4
    for pair in range(NF // 2):
        part = jnp.concatenate([spectra[q, 16 * pair : 16 * pair + 16, :] for q in range(NQ)], axis=0)
        r0, i0, r1, i1, tail = (part[:, 128 * k : 128 * k + 128] for k in range(5))
        rt, it = tail[:, :64], tail[:, 64:]
        left = jnp.concatenate(
            [
                jnp.concatenate([r0, -i0, r1, -i1, rt, -it], axis=1),
                jnp.concatenate([i0, r0, i1, r1, it, rt], axis=1),
            ],
            axis=0,
        )
        low = jnp.dot(left, w_p[2 * pair], preferred_element_type=F32)
        high = jnp.dot(left, w_p[2 * pair + 1], preferred_element_type=F32)
        both = jnp.where(even, low, high).reshape(2 * NQ, 2, 8, NG)
        own[pair] = both[:, 0]
        give[pair] = both[:, 1].astype(BF)
        copy = pltpu.make_async_remote_copy(
            src_ref=give.at[pair], dst_ref=take.at[pair], send_sem=core_send.at[pair], recv_sem=core_recv.at[pair],
            device_id=(param_at(0, 0, 1), qj), device_id_type=MESH,
        )
        copy.start()
        core_copies.append(copy)

    for pair in range(NF // 2):
        core_copies[pair].wait()
        for k in range(2):
            for q in range(NQ):
                total = own[pair, k * NQ + q] + take[pair, k * NQ + q].astype(F32)
                for half in range(2):
                    spread[q, half, pl.ds(k * 4 + pair, 8, 8), :] = total[:, 128 * half : 128 * half + 128]
    for q in range(NQ):
        for half in range(2):
            send[q, :, :, :, 128 * half : 128 * half + 128] = spread[q, half].reshape(2, 4, 8, 128).astype(BF)

    pl.semaphore_wait(line, 1)
    for dx, dz in owner_offsets():
        px, pz = (xh + dx) % NX, (z + dz + NZ) % NZ
        pltpu.make_async_remote_copy(
            src_ref=send.at[px * 4 + pz // 4, :, pz % 4], dst_ref=recv.at[chip], send_sem=rs_send, recv_sem=rs_recv,
            device_id=((px * NZ + pz) * 2 + core, qj), device_id_type=MESH,
        ).start()

    mine = xh * 4 + z // 4
    at = pl.multiple_of((z % 4) * 8, 8)
    acc0, acc1 = (
        jnp.concatenate([spread[mine, half, pl.ds(at + shift, 8), :] for half in range(2)], axis=1) for shift in (0, 32)
    )
    recv[chip] = jnp.zeros((2, 8, NG), BF)
    group_copy.wait()
    onehot = (lax.broadcasted_iota(jnp.int32, (128, NG), 0) == group_v[...]).astype(F32)

    pltpu.make_async_copy(recv.at[pl.ds(0, 31)], recv.at[pl.ds(0, 31)], rs_recv).wait()
    got = jnp.sum(recv[...].astype(F32), axis=0)
    total = jnp.concatenate([acc0 + got[0], acc1 + got[1]], axis=0)
    acc_out[...] = total
    segs[qj] = lax.dot_general(
        total, onehot, (((1,), (1,)), ((), ())), precision=lax.Precision.HIGHEST, preferred_element_type=F32
    )
    seg = [
        pltpu.make_async_remote_copy(
            src_ref=segs.at[qj], dst_ref=segs.at[qj], send_sem=seg_send.at[d - 1], recv_sem=seg_recv.at[d - 1],
            device_id=(pi, (qj + d) % NQ), device_id_type=MESH,
        )
        for d in range(1, NQ)
    ]
    for copy in seg:
        copy.start()
    pltpu.make_async_copy(recv.at[pl.ds(0, 31)], recv.at[pl.ds(0, 31)], rs_send).wait()
    for copy in seg:
        copy.wait()
    seg_out[...] = jnp.sum(segs[...], axis=0) * math.sqrt(GROUPS / (NG * NQ))


def local(samples, operator_rows, block_start, gauge_group):
    anywhere = pl.BlockSpec(memory_space=pl.ANY)
    in_vmem = pl.BlockSpec(memory_space=pltpu.VMEM)
    dma = pltpu.SemaphoreType.DMA
    acc, seg = pl.pallas_call(
        kernel,
        out_shape=(jax.ShapeDtypeStruct((16, NG), F32), jax.ShapeDtypeStruct((16, 128), F32)),
        in_specs=[anywhere] * 4,
        out_specs=(in_vmem, in_vmem),
        scratch_shapes=[
            pltpu.VMEM((NT, NS, NP), BF),
            pltpu.VMEM((256, NT * NS), BF),
            pltpu.VMEM((2, NF, NT * NS), F32),
            pltpu.VMEM((NF, NP, 2, NG), BF),
            pltpu.VMEM((NF, LANES, NG), BF),
            pltpu.VMEM((2, 256, 256), BF),
            pltpu.VMEM((NQ, 64, LANES), BF),
            pltpu.VMEM((4, 2 * NQ, 8, NG), BF),
            pltpu.VMEM((4, 2 * NQ, 8, NG), BF),
            pltpu.VMEM((4, 2 * NQ, 8, NG), F32),
            pltpu.VMEM((NQ, 2, 64, 128), F32),
            pltpu.VMEM((NQ, 2, 4, 8, NG), BF),
            pltpu.VMEM((NX * NZ, 2, 8, NG), BF),
            pltpu.VMEM((NQ, 16, 128), F32),
            pltpu.SMEM((1,), jnp.int32),
            pltpu.VMEM((1, NG), jnp.int32),
            dma((len(STEPS),)),
            dma,
            dma,
            dma,
            dma((NQ - 1,)),
            dma((NQ - 1,)),
            dma((4,)),
            dma((4,)),
            dma,
            dma,
            dma((NQ - 1,)),
            dma((NQ - 1,)),
            pltpu.SemaphoreType.REGULAR,
            pltpu.SemaphoreType.REGULAR,
        ],
        compiler_params=pltpu.CompilerParams(collective_id=0, has_side_effects=True),
    )(samples.transpose(2, 0, 1), operator_rows, block_start, gauge_group.reshape(1, NG))
    response = acc.reshape(2, 2, 4, NG).transpose(1, 2, 0, 3).reshape(1, 2, NF, NG)
    segment = seg[:, :GROUPS].reshape(2, 2, 4, GROUPS).transpose(1, 2, 0, 3).reshape(1, 2, NF, GROUPS)
    return response, segment


def solution(mesh):
    return jax.shard_map(
        local,
        mesh=mesh,
        in_specs=(P("qoi", "param", None), P(None, "param", None, "qoi"), P(), P("qoi")),
        out_specs=(P("param", None, None, "qoi"), P("param", None, None, None)),
        check_vma=False,
    )
```

time: 90 us -> 50.8 us (0.56)
  the two profiles are of different devices: /device:TPU:1 before, /device:TPU:2 now
where the time goes in v1:
time: 50.8 us; the launch traced here: 50.5 us
  Pallas kernels  46.5 us (92%)
  local copies, waits for them, and re-layouts  2.66 us (5%)
  between operations  1.29 us (3%)
    pallas_call x1, Pallas kernels, local(): pl.pallas_call(kernel, out_shape=(jax.ShapeDtypeStruct((16, NG), F32), ja...  46.5 us
    reshape x2, local copies, waits for them, and re-layouts, local(): acc.reshape(2, 2, 4, NG).transpose(1, 2, 0, 3).reshape(1, 2, NF, NG)  1.35 us
    transpose x1, local copies, waits for them, and re-layouts, local(): seg[:, :GROUPS].reshape(2, 2, 4, GROUPS).transpose(1, 2, 0, 3)  1.3 us

profile of v1, /device:TPU:2, one launch (start us, length us, event | category | flops | bytes accessed | tf_op | source)
XLA Modules:
  0.0 50.5 jit_solution(5308027925711613089)
XLA Ops:
  1.3 46.5 %shard_map.59 = (f32[16,256]{1,0:T(8,128)}, f32[16,128]{1,0:T(8,128)}) custom-call(bf16[420,8,320]{2,1,0:T(8,128)(2,1)} %bitcast.8, bf16[8,320,2,256]{3,2,1,0:T(2,128)(2,1)} %w_hbm.1, s32[1]{0:T(128)S(6)} %copy.8.first_hbm, s32[1,256]{1,0:T(1,128)} %bitcast.12), custom_call_target="tpu_custom_call" | custom-call | tf_op jit(solution)/shard_map/pallas_call | solution.py:241
  47.8 0.7 %reshape.20 = f32[2,2,4,256]{3,2,1,0:T(4,128)S(1)} reshape(f32[16,256]{1,0:T(8,128)} %get-tuple-element.4) | data formatting | bytes 32768 | tf_op jit(solution)/shard_map/reshape | solution.py:280
  48.5 0.6 %reshape.21 = f32[1,2,8,256]{3,2,1,0:T(8,128)} reshape(f32[2,4,2,256]{3,2,1,0:T(2,128)S(1)} %copy.6) | data formatting | bytes 32768 | tf_op jit(solution)/shard_map/reshape | solution.py:280
  49.2 1.3 %copy.7 = f32[2,4,2,16]{3,2,1,0:T(2,128)} copy(f32[2,4,2,16]{3,1,0,2:T(4,128)} %bitcast.10) | data formatting | bytes 2048 | tf_op jit(solution)/shard_map/transpose | solution.py:281
  (1 shorter events, 0.0 us)

commit v2 on v1

v2 whole, which is shorter than its diff:
```python
import math

import jax
import jax.numpy as jnp
from jax import lax
from jax.experimental import pallas as pl
from jax.experimental.pallas import tpu as pltpu
from jax.sharding import PartitionSpec as P

GROUPS = 16
MESH = pl.DeviceIdType.MESH
BF = jnp.bfloat16
F32 = jnp.float32

NQ = 8
NX = 2
NZ = 16
NF = 8
NT = 420
NS = 8
NP = 320
NG = 256
LANES = 2 * NP
WIDE = 512
TABLE = -(-NT * NS // WIDE) * WIDE
STEPS = ((0, 132), (132, 160), (292, 128))
CUBE = 4
NC = 4
PC = NF // 2 // NC
RB = 4 * PC
scope = jax.named_scope


def rank_of(cube):
    return cube + (cube == 2).astype(jnp.int32) - (cube == 3).astype(jnp.int32)


def owner_offsets():
    return sorted((dz for dz in range(-NZ // 2 + 1, NZ // 2 + 1) if dz), key=lambda dz: (-abs(dz), -dz))


def phase_rows(first, begin, width):
    lane = lax.broadcasted_iota(jnp.int32, (NF, width), 1) + begin
    freq = lax.broadcasted_iota(jnp.int32, (NF, width), 0) + first
    turns = ((lane >> 3) * freq).astype(F32)
    rest = turns - NT * jnp.floor(turns * (1.0 / NT))
    quarter = jnp.floor(rest * (4.0 / NT) + 0.5)
    angle = (rest - (NT // 4) * quarter) * (2.0 * math.pi / NT)
    sq = angle * angle
    sine = angle * (1.0 + sq * (-1.0 / 6 + sq * (1.0 / 120 + sq * (-1.0 / 5040 + sq * (1.0 / 362880)))))
    cosine = 1.0 + sq * (-0.5 + sq * (1.0 / 24 + sq * (-1.0 / 720 + sq * (1.0 / 40320 + sq * (-1.0 / 3628800)))))
    odd = (quarter == 1.0) | (quarter == 3.0)
    scale = 1.0 / math.sqrt(NT)
    cos_all = jnp.where(odd, sine, cosine) * jnp.where((quarter == 1.0) | (quarter == 2.0), -scale, scale)
    sin_all = jnp.where(odd, cosine, sine) * jnp.where((quarter == 2.0) | (quarter == 3.0), scale, -scale)
    return cos_all, sin_all


def fill_table(first, core, rows_ref, table_ref):
    def step(i, carry):
        begin = pl.multiple_of(i * WIDE, WIDE)
        span = pl.ds(begin, WIDE)
        rows_ref[0], rows_ref[1] = phase_rows(first, begin, WIDE)
        sample = lax.broadcasted_iota(jnp.int32, (16, WIDE), 1) % NS
        row = lax.broadcasted_iota(jnp.int32, (16, WIDE), 0)
        side = jnp.where(row < 8, core, 1 - core)
        hit = sample == ((row % 8) // 2) * 2 + side
        upper = row % 2 == 1
        for part in range(2):
            for pair in range(NF // 2):
                low = jnp.broadcast_to(rows_ref[part, 2 * pair : 2 * pair + 1], (16, WIDE))
                high = jnp.broadcast_to(rows_ref[part, 2 * pair + 1 : 2 * pair + 2], (16, WIDE))
                value = jnp.where(hit, jnp.where(upper, high, low), 0.0)
                rounded = value.astype(BF)
                at = part * 64 + pair * 16
                table_ref[at : at + 16, span] = rounded
                table_ref[128 + at : 144 + at, span] = (value - rounded.astype(F32)).astype(BF)
        return carry

    lax.fori_loop(0, TABLE // WIDE, step, 0)


def diagonal(shape):
    return lax.broadcasted_iota(jnp.int32, shape, 2) // GROUPS == lax.broadcasted_iota(jnp.int32, shape, 1)


def planar(f, w_ref, order_ref, out_ref):
    for begin in range(0, NP, 128):
        count = min(128, NP - begin)
        rows = w_ref[f, begin : begin + count].reshape(2 * count, NG)
        order = order_ref[0] if count == 128 else order_ref[1, : 2 * count, : 2 * count]
        out_ref[f, 2 * begin : 2 * (begin + count)] = jnp.dot(order, rows, preferred_element_type=F32).astype(BF)


def kernel(
    x_hbm, w_hbm, first_ref, group_hbm, acc_out, seg_out,
    x_v, table, rows, w_v, w_p, order, spectra, give, take, own, x_give, x_take, kept, spread, send, recv, segs, group_v,
    x_sem, w_sem, group_sem, ag_send, ag_recv, core_send, core_recv, x_send, x_recv, rs_send, rs_recv, seg_send, seg_recv,
    around, above,
):
    pi, qj = lax.axis_index("param"), lax.axis_index("qoi")
    core, chip = pi % 2, pi // 2
    xh, z = chip // NZ, chip % NZ

    def param_at(dx, dz, dc=0):
        return (((xh + dx) % NX) * NZ + (z + dz + NZ) % NZ) * 2 + (core + dc) % 2

    with scope("begin"):
        x_copies = [
            pltpu.make_async_copy(x_hbm.at[pl.ds(t0, n)], x_v.at[pl.ds(t0, n)], x_sem.at[i])
            for i, (t0, n) in enumerate(STEPS)
        ]
        w_copy = pltpu.make_async_copy(w_hbm, w_v, w_sem)
        group_copy = pltpu.make_async_copy(group_hbm, group_v, group_sem)
        for copy in x_copies:
            copy.start()

    place, cube = z % CUBE, z // CUBE
    rank = rank_of(cube)
    plane = [(param_at(1, 0), qj), (param_at(0, 0, 1), qj)] + [(pi, (qj + d) % NQ) for d in range(1, NQ)]
    within = [(((xh * NZ) + cube * CUBE + (place + d) % CUBE) * 2 + core, qj) for d in range(1, CUBE)]
    others = [((cube + d) % (NZ // CUBE), (param_at(0, CUBE * d), qj)) for d in range(1, NZ // CUBE)]
    with scope("signals"):
        barrier = pltpu.get_barrier_semaphore()
        for peer in plane + within:
            pl.semaphore_signal(barrier, inc=1, device_id=peer, device_id_type=MESH)
        for other, peer in others:
            @pl.when(rank_of(other) > rank)
            def _():
                pl.semaphore_signal(barrier, inc=1, device_id=peer, device_id_type=MESH)

    with scope("table"):
        fill_table(first_ref[0], core, rows, table)
        w_copy.start()
        group_copy.start()

    with scope("dft"):
        halves = None
        for copy, (t0, n) in zip(x_copies, STEPS):
            with scope("xw"):
                copy.wait()
            steps = x_v[t0 : t0 + n].reshape(n * NS, NP)
            term = jnp.dot(table[:, t0 * NS : (t0 + n) * NS], steps, preferred_element_type=F32)
            halves = term if halves is None else halves + term
        spectrum = (halves[:128] + halves[128:]).astype(BF)
        real, imag = spectrum[:64], spectrum[64:]
        for block in range(2):
            spectra[qj, :, 256 * block : 256 * block + 128] = real[:, 128 * block : 128 * block + 128]
            spectra[qj, :, 256 * block + 128 : 256 * block + 256] = imag[:, 128 * block : 128 * block + 128]
        spectra[qj, :, 512:640] = jnp.concatenate([real[:, 256:320], imag[:, 256:320]], axis=1)

    def ag_copy(c, d):
        block = spectra.at[qj, pl.ds(pl.multiple_of(16 * PC * c, 16 * PC), 16 * PC)]
        return pltpu.make_async_remote_copy(
            src_ref=block, dst_ref=block, send_sem=ag_send, recv_sem=ag_recv.at[c],
            device_id=(pi, (qj + d) % NQ), device_id_type=MESH,
        )

    def ag_all(c):
        return spectra.at[pl.ds(0, NQ - 1), pl.ds(pl.multiple_of(16 * PC * c, 16 * PC), 16 * PC)]

    with scope("near"):
        pl.semaphore_wait(barrier, len(plane) + len(within) + rank)
    with scope("ag_start"):
        def ag_step(c, carry):
            for d in range(1, NQ):
                ag_copy(c, d).start()
            return carry

        lax.fori_loop(0, NC, ag_step, 0)
        for peer in within:
            pl.semaphore_signal(around, inc=1, device_id=peer, device_id_type=MESH)

    def planar_step(f, carry):
        planar(f, w_v, order, w_p)
        return carry

    with scope("planar0"):
        big = lax.broadcasted_iota(jnp.int32, (256, 256), 0)
        col = lax.broadcasted_iota(jnp.int32, (256, 256), 1)
        order[0] = jnp.where(col == (big % 128) * 2 + big // 128, 1.0, 0.0).astype(BF)
        order[1] = jnp.where(col == (big % 64) * 2 + (big // 64) % 2, 1.0, 0.0).astype(BF)
        w_copy.wait()
        lax.fori_loop(0, NF // 2, planar_step, 0)
    with scope("around"):
        pl.semaphore_wait(around, len(within))
        for other, peer in others:
            @pl.when(rank_of(other) < rank)
            def _():
                pl.semaphore_signal(above, inc=1, device_id=peer, device_id_type=MESH)

    with scope("planar1"):
        lax.fori_loop(NF // 2, NF, planar_step, 0)
        group_copy.wait()

    even = (lax.broadcasted_iota(jnp.int32, (256, NG), 0) % 2) == 0

    def core_copy(pair):
        return pltpu.make_async_remote_copy(
            src_ref=give.at[pair], dst_ref=take.at[pair], send_sem=core_send, recv_sem=core_recv.at[pair],
            device_id=(param_at(0, 0, 1), qj), device_id_type=MESH,
        )

    def product(pair):
        at = pl.multiple_of(16 * pair, 16)
        part = jnp.concatenate([spectra[q, pl.ds(at, 16), :] for q in range(NQ)], axis=0)
        r0, i0, r1, i1, tail = (part[:, 128 * k : 128 * k + 128] for k in range(5))
        rt, it = tail[:, :64], tail[:, 64:]
        left = jnp.concatenate(
            [
                jnp.concatenate([r0, -i0, r1, -i1, rt, -it], axis=1),
                jnp.concatenate([i0, r0, i1, r1, it, rt], axis=1),
            ],
            axis=0,
        )
        low = jnp.dot(left, w_p[2 * pair], preferred_element_type=F32)
        high = jnp.dot(left, w_p[2 * pair + 1], preferred_element_type=F32)
        both = jnp.where(even, low, high).reshape(2 * NQ, 2, 8, NG)
        give[pair] = both[:, 1].astype(BF)
        core_copy(pair).start()
        own[pair] = both[:, 0]

    half_q = NQ // NX

    def x_copy(c):
        return pltpu.make_async_remote_copy(
            src_ref=x_give.at[c], dst_ref=x_take.at[c], send_sem=x_send, recv_sem=x_recv.at[c],
            device_id=(param_at(1, 0), qj), device_id_type=MESH,
        )

    def across(c):
        for p in range(PC):
            pair = c * PC + p
            with scope("core_wait"):
                core_copy(pair).wait_recv()
            for k in range(2):
                at = k * NQ + (1 - xh) * half_q
                x_give[c, p, k] = (own[pair, pl.ds(at, half_q)] + take[pair, pl.ds(at, half_q)].astype(F32)).astype(BF)
        x_copy(c).start()
        for p in range(PC):
            pair = c * PC + p
            for k in range(2):
                at = k * NQ + xh * half_q
                kept[c, p, k] = own[pair, pl.ds(at, half_q)] + take[pair, pl.ds(at, half_q)].astype(F32)

    def sums(c):
        with scope("x_wait"):
            x_copy(c).wait_recv()
        for q in range(half_q):
            for p in range(PC):
                for k in range(2):
                    total = kept[c, p, k, q] + x_take[c, p, k, q].astype(F32)
                    for half in range(2):
                        spread[c, q, half, pl.ds(k * PC + p, 8, 2 * PC), :] = total[:, 128 * half : 128 * half + 128]
        for q in range(half_q):
            for half in range(2):
                send[c, q, :, :, 128 * half : 128 * half + 128] = spread[c, q, half].reshape(4, RB, 128).astype(BF)

    def give_out(c, later):
        for dz in owner_offsets():
            pz = (z + dz + NZ) % NZ
            known = rank_of(pz // CUBE) <= rank

            @pl.when(jnp.logical_not(known) if later else known)
            def _():
                pltpu.make_async_remote_copy(
                    src_ref=send.at[c, pz // 4, pz % 4], dst_ref=recv.at[c, z],
                    send_sem=rs_send, recv_sem=rs_recv.at[c],
                    device_id=(param_at(0, dz), qj), device_id_type=MESH,
                ).start()
        if not later:
            recv[c, z] = jnp.zeros((RB, NG), BF)

    for c in range(NC):
        with scope(f"ag_wait{c}"):
            pltpu.make_async_copy(ag_all(c), ag_all(c), ag_recv.at[c]).wait()
        with scope(f"products{c}"):
            for p in range(PC):
                product(c * PC + p)
        if c > 0:
            with scope(f"across{c - 1}"):
                across(c - 1)
    with scope(f"across{NC - 1}"):
        across(NC - 1)
    for c in range(NC):
        with scope(f"sums{c}"):
            sums(c)
        with scope(f"rs_start{c}"):
            give_out(c, False)

    @pl.when(rank < NZ // CUBE - 1)
    def _():
        with scope("above"):
            pl.semaphore_wait(above, NZ // CUBE - 1 - rank)
        with scope("rs_later"):
            for c in range(NC):
                give_out(c, True)

    mine = z // 4
    onehot = (lax.broadcasted_iota(jnp.int32, (128, NG), 0) % GROUPS == group_v[...]).astype(F32)
    for c in range(NC):
        with scope(f"rs_wait{c}"):
            whole = recv.at[c, pl.ds(0, NZ - 1)]
            pltpu.make_async_copy(whole, whole, rs_recv.at[c]).wait()
        with scope(f"final{c}"):
            at = pl.multiple_of((z % 4) * RB, RB)
            here = jnp.concatenate([spread[c, mine, half, pl.ds(at, RB), :] for half in range(2)], axis=1)
            total = here + jnp.sum(recv[c].astype(F32), axis=0)
            for f2 in range(2):
                for k in range(2):
                    for p in range(PC):
                        row = (f2 * 2 + k) * PC + p
                        acc_out[k, (c * PC + p) * 2 + f2 : (c * PC + p) * 2 + f2 + 1, :] = total[row : row + 1]
    with scope("segment"):
        grouped = lax.dot_general(
            acc_out[...].reshape(16, NG), onehot, (((1,), (1,)), ((), ())),
            precision=lax.Precision.HIGHEST, preferred_element_type=F32,
        )
        segs[qj] = jnp.sum(jnp.where(diagonal((2, NF, 128)), grouped.reshape(2, NF, 128), 0.0), axis=1)
        seg = [
            pltpu.make_async_remote_copy(
                src_ref=segs.at[qj], dst_ref=segs.at[qj], send_sem=seg_send, recv_sem=seg_recv,
                device_id=(pi, (qj + d) % NQ), device_id_type=MESH,
            )
            for d in range(1, NQ)
        ]
        for copy in seg:
            copy.start()
    with scope("send_waits"):
        whole = recv.at[:, pl.ds(0, NZ - 1)]
        pltpu.make_async_copy(whole, whole, rs_send).wait()
        sent = spectra.at[pl.ds(0, NQ - 1)]
        pltpu.make_async_copy(sent, sent, ag_send).wait()
        pltpu.make_async_copy(give, give, core_send).wait()
        pltpu.make_async_copy(x_give, x_give, x_send).wait()
    with scope("seg_wait"):
        pltpu.make_async_copy(segs.at[pl.ds(0, NQ - 1)], segs.at[pl.ds(0, NQ - 1)], seg_recv).wait()
        pltpu.make_async_copy(segs.at[pl.ds(0, NQ - 1)], segs.at[pl.ds(0, NQ - 1)], seg_send).wait()
    seg_out[...] = jnp.sum(segs[...], axis=0) * math.sqrt(GROUPS / (NG * NQ))


def finish(acc_ref, seg_ref, response_ref, segment_ref):
    response_ref[0] = acc_ref[...]
    for f in range(NF):
        segment_ref[0, :, f, :] = seg_ref[:, GROUPS * f : GROUPS * (f + 1)]


def local(samples, operator_rows, block_start, gauge_group):
    in_hbm = pl.BlockSpec(memory_space=pltpu.HBM)
    in_vmem = pl.BlockSpec(memory_space=pltpu.VMEM)
    dma = pltpu.SemaphoreType.DMA
    acc, seg = pl.pallas_call(
        kernel,
        out_shape=(pltpu.VMEM((2, NF, NG), F32), pltpu.VMEM((2, 128), F32)),
        in_specs=[in_hbm, in_hbm, pl.BlockSpec(memory_space=pltpu.SMEM), in_hbm],
        out_specs=(in_vmem, in_vmem),
        scratch_shapes=[
            pltpu.VMEM((NT, NS, NP), BF),
            pltpu.VMEM((256, TABLE), BF),
            pltpu.VMEM((2, NF, WIDE), F32),
            pltpu.VMEM((NF, NP, 2, NG), BF),
            pltpu.VMEM((NF, LANES, NG), BF),
            pltpu.VMEM((2, 256, 256), BF),
            pltpu.VMEM((NQ, 64, LANES), BF),
            pltpu.VMEM((4, 2 * NQ, 8, NG), BF),
            pltpu.VMEM((4, 2 * NQ, 8, NG), BF),
            pltpu.VMEM((4, 2 * NQ, 8, NG), F32),
            pltpu.VMEM((NC, PC, 2, NQ // NX, 8, NG), BF),
            pltpu.VMEM((NC, PC, 2, NQ // NX, 8, NG), BF),
            pltpu.VMEM((NC, PC, 2, NQ // NX, 8, NG), F32),
            pltpu.VMEM((NC, NQ // NX, 2, 8 * 2 * PC, 128), F32),
            pltpu.VMEM((NC, NQ // NX, 4, RB, NG), BF),
            pltpu.VMEM((NC, NZ, RB, NG), BF),
            pltpu.VMEM((NQ, 2, 128), F32),
            pltpu.VMEM((1, NG), jnp.int32),
            dma((len(STEPS),)),
            dma,
            dma,
            dma,
            dma((NC,)),
            dma,
            dma((4,)),
            dma,
            dma((NC,)),
            dma,
            dma((NC,)),
            dma,
            dma,
            pltpu.SemaphoreType.REGULAR,
            pltpu.SemaphoreType.REGULAR,
        ],
        compiler_params=pltpu.CompilerParams(collective_id=0, has_side_effects=True),
    )(samples.transpose(2, 0, 1), operator_rows, block_start, gauge_group.reshape(1, NG))
    return pl.pallas_call(
        finish,
        out_shape=(jax.ShapeDtypeStruct((1, 2, NF, NG), F32), jax.ShapeDtypeStruct((1, 2, NF, GROUPS), F32)),
        in_specs=[in_vmem] * 2,
        out_specs=(in_vmem, in_vmem),
    )(pltpu.with_memory_space_constraint(acc, pltpu.VMEM), pltpu.with_memory_space_constraint(seg, pltpu.VMEM))


def solution(mesh):
    return jax.shard_map(
        local,
        mesh=mesh,
        in_specs=(P("qoi", "param", None), P(None, "param", None, "qoi"), P(), P("qoi")),
        out_specs=(P("param", None, None, "qoi"), P("param", None, None, None)),
        check_vma=False,
    )
```

time: 50.8 us -> 42.9 us (0.84)
  Pallas kernels: 46.5 us -> 41.5 us
  local copies, waits for them, and re-layouts: 2.66 us -> 0 us
    pallas_call x1 -> x2, Pallas kernels: 46.5 us -> 41.5 us  [the longest x1 40.8 us: local(): pl.pallas_call(kernel, out_shape=(pltpu.VMEM((2, NF, NG), F32), pltpu.VME...]
    reshape x2 -> x0, local copies, waits for them, and re-layouts: 1.35 us -> none  [local(): acc.reshape(2, 2, 4, NG).transpose(1, 2, 0, 3).reshape(1, 2, NF, NG)]
    transpose x2 -> x0, local copies, waits for them, and re-layouts: 1.31 us -> none  [the longest x1 1.3 us: local(): seg[:, :GROUPS].reshape(2, 2, 4, GROUPS).transpose(1, 2, 0, 3)]
where the time goes in v2:
time: 42.9 us; the launch traced here: 42.7 us
  Pallas kernels  41.5 us (97%)
  between operations  1.28 us (3%)
    pallas_call x1, Pallas kernels, local(): pl.pallas_call(kernel, out_shape=(pltpu.VMEM((2, NF, NG), F32), pltpu.VME...  40.8 us

profile of v2, /device:TPU:2, one launch (start us, length us, event | category | flops | bytes accessed | tf_op | source)
XLA Modules:
  0.0 42.7 jit_solution(5684299009676226866)
XLA Ops:
  1.3 40.8 %shard_map.59 = (f32[2,8,256]{2,1,0:T(8,128)S(1)}, f32[2,128]{1,0:T(2,128)S(1)}) custom-call(bf16[420,8,320]{2,1,0:T(8,128)(2,1)} %bitcast.2, bf16[8,320,2,256]{3,2,1,0:T(2,128)(2,1)} %w_hbm.1, s32[1]{0:T(128)S(6)} %copy.6.first_ref, s32[1,256]{1,0:T(1,128)} %bitcast.3), custom_call_target="tpu_custom_call" | custom-call | tf_op jit(solution)/shard_map/pallas_call | solution.py:352
  42.1 0.7 %shard_map.60 = (f32[1,2,8,256]{3,2,1,0:T(8,128)}, f32[1,2,8,16]{3,2,1,0:T(8,128)}) custom-call(f32[2,8,256]{2,1,0:T(8,128)S(1)} %get-tuple-element.4.acc_ref, f32[2,128]{1,0:T(2,128)S(1)} %get-tuple-element.5.seg_ref), custom_call_target="tpu_custom_call" | custom-call | tf_op jit(solution)/shard_map/pallas_call | solution.py:394

commit v3 on v2

--- a/solution.py
+++ b/solution.py
@@ -13,6 +13,7 @@
 F32 = jnp.float32
 
 NQ = 8
+NY = 4
 NX = 2
 NZ = 16
 NF = 8
@@ -23,11 +24,15 @@
 LANES = 2 * NP
 WIDE = 512
 TABLE = -(-NT * NS // WIDE) * WIDE
-STEPS = ((0, 132), (132, 160), (292, 128))
+STEPS = ((0, 68), (68, 128), (196, 128), (324, 96))
 CUBE = 4
 NC = 4
 PC = NF // 2 // NC
 RB = 4 * PC
+ROUTES = "xyxy"
+STAGED = 3
+SLOTS = STAGED * NZ + (NC - STAGED) * NX * NZ
+ARRIVALS = STAGED * (NZ - 1) + (NC - STAGED) * (NX * NZ - 1)
 scope = jax.named_scope
 
 
@@ -35,8 +40,9 @@
     return cube + (cube == 2).astype(jnp.int32) - (cube == 3).astype(jnp.int32)
 
 
-def owner_offsets():
-    return sorted((dz for dz in range(-NZ // 2 + 1, NZ // 2 + 1) if dz), key=lambda dz: (-abs(dz), -dz))
+def owner_offsets(lines):
+    pairs = [(dx, dz) for dx in range(lines) for dz in range(-NZ // 2 + 1, NZ // 2 + 1) if (dx, dz) != (0, 0)]
+    return sorted(pairs, key=lambda pair: (-(abs(pair[1]) + 2 * pair[0]), -pair[1]))
 
 
 def phase_rows(first, begin, width):
@@ -95,8 +101,8 @@
 def kernel(
     x_hbm, w_hbm, first_ref, group_hbm, acc_out, seg_out,
     x_v, table, rows, w_v, w_p, order, spectra, give, take, own, x_give, x_take, kept, spread, send, recv, segs, group_v,
-    x_sem, w_sem, group_sem, ag_send, ag_recv, core_send, core_recv, x_send, x_recv, rs_send, rs_recv, seg_send, seg_recv,
-    around, above,
+    x_sem, w_sem, group_sem, ag_send, ag_first, ag_recv, core_send, core_recv, x_send, x_recv, rs_send, rs_recv, seg_send, seg_recv,
+    around, line, above,
 ):
     pi, qj = lax.axis_index("param"), lax.axis_index("qoi")
     core, chip = pi % 2, pi // 2
@@ -137,8 +143,7 @@
     with scope("dft"):
         halves = None
         for copy, (t0, n) in zip(x_copies, STEPS):
-            with scope("xw"):
-                copy.wait()
+            copy.wait()
             steps = x_v[t0 : t0 + n].reshape(n * NS, NP)
             term = jnp.dot(table[:, t0 * NS : (t0 + n) * NS], steps, preferred_element_type=F32)
             halves = term if halves is None else halves + term
@@ -149,25 +154,47 @@
             spectra[qj, :, 256 * block + 128 : 256 * block + 256] = imag[:, 128 * block : 128 * block + 128]
         spectra[qj, :, 512:640] = jnp.concatenate([real[:, 256:320], imag[:, 256:320]], axis=1)
 
-    def ag_copy(c, d):
-        block = spectra.at[qj, pl.ds(pl.multiple_of(16 * PC * c, 16 * PC), 16 * PC)]
+    xl, y = qj // NY, qj % NY
+    beside = (1 - xl) * NY + y
+    along = [xl * NY + (y + d) % NY for d in range(1, NY)]
+
+    def chunk_of(q, c):
+        return spectra.at[q, pl.ds(16 * PC * c, 16 * PC)]
+
+    def ag_copy(q, c, peer, sem):
         return pltpu.make_async_remote_copy(
-            src_ref=block, dst_ref=block, send_sem=ag_send, recv_sem=ag_recv.at[c],
-            device_id=(pi, (qj + d) % NQ), device_id_type=MESH,
+            src_ref=chunk_of(q, c), dst_ref=chunk_of(q, c), send_sem=ag_send, recv_sem=sem.at[c],
+            device_id=(pi, peer), device_id_type=MESH,
         )
 
-    def ag_all(c):
-        return spectra.at[pl.ds(0, NQ - 1), pl.ds(pl.multiple_of(16 * PC * c, 16 * PC), 16 * PC)]
+    def await_blocks(count, c, sem):
+        blocks = spectra.at[pl.ds(0, count), pl.ds(16 * PC * c, 16 * PC)]
+        pltpu.make_async_copy(blocks, blocks, sem.at[c]).wait()
+
+    def hand_on(c):
+        if ROUTES[c] == "x":
+            await_blocks(1, c, ag_first)
+            for peer in along:
+                ag_copy(beside, c, peer, ag_recv).start()
+        if ROUTES[c] == "y":
+            await_blocks(NY - 1, c, ag_first)
+            for q in along:
+                ag_copy(q, c, beside, ag_recv).start()
+
+    def ag_wait(c):
+        await_blocks({"d": NQ - 1, "x": 2 * (NY - 1), "y": NY}[ROUTES[c]], c, ag_recv)
 
     with scope("near"):
         pl.semaphore_wait(barrier, len(plane) + len(within) + rank)
     with scope("ag_start"):
-        def ag_step(c, carry):
-            for d in range(1, NQ):
-                ag_copy(c, d).start()
-            return carry
-
-        lax.fori_loop(0, NC, ag_step, 0)
+        for c in sorted(range(NC), key=lambda c: ROUTES[c] != "x"):
+            ag_copy(qj, c, beside, ag_first if ROUTES[c] == "x" else ag_recv).start()
+        for c in sorted(range(NC), key=lambda c: ROUTES[c] == "x"):
+            for peer in along:
+                ag_copy(qj, c, peer, ag_first if ROUTES[c] == "y" else ag_recv).start()
+            if ROUTES[c] == "d":
+                for d in range(1, NY):
+                    ag_copy(qj, c, (1 - xl) * NY + (y + d) % NY, ag_recv).start()
         for peer in within:
             pl.semaphore_signal(around, inc=1, device_id=peer, device_id_type=MESH)
 
@@ -184,14 +211,27 @@
         lax.fori_loop(0, NF // 2, planar_step, 0)
     with scope("around"):
         pl.semaphore_wait(around, len(within))
+        pl.semaphore_signal(line, inc=1, device_id=(param_at(1, 0), qj), device_id_type=MESH)
+    with scope("hand0"):
+        for c in range(NC):
+            if ROUTES[c] == "x":
+                hand_on(c)
+    with scope("planar1"):
+        lax.fori_loop(NF // 2, NF * 3 // 4, planar_step, 0)
+    with scope("hand1"):
+        hand_on(1)
+    with scope("planar2"):
+        lax.fori_loop(NF * 3 // 4, NF, planar_step, 0)
+        group_copy.wait()
+    with scope("hand3"):
+        hand_on(3)
+
+    with scope("line"):
+        pl.semaphore_wait(line, 1)
         for other, peer in others:
             @pl.when(rank_of(other) < rank)
             def _():
                 pl.semaphore_signal(above, inc=1, device_id=peer, device_id_type=MESH)
-
-    with scope("planar1"):
-        lax.fori_loop(NF // 2, NF, planar_step, 0)
-        group_copy.wait()
 
     even = (lax.broadcasted_iota(jnp.int32, (256, NG), 0) % 2) == 0
 
@@ -243,50 +283,81 @@
                 at = k * NQ + xh * half_q
                 kept[c, p, k] = own[pair, pl.ds(at, half_q)] + take[pair, pl.ds(at, half_q)].astype(F32)
 
-    def sums(c):
-        with scope("x_wait"):
-            x_copy(c).wait_recv()
-        for q in range(half_q):
+    def lay(c, first, count, total):
+        for q in range(count):
             for p in range(PC):
                 for k in range(2):
-                    total = kept[c, p, k, q] + x_take[c, p, k, q].astype(F32)
+                    value = total(p, k, q)
                     for half in range(2):
-                        spread[c, q, half, pl.ds(k * PC + p, 8, 2 * PC), :] = total[:, 128 * half : 128 * half + 128]
-        for q in range(half_q):
+                        spread[first + q, half, pl.ds(k * PC + p, 8, 2 * PC), :] = value[:, 128 * half : 128 * half + 128]
+        for q in range(count):
             for half in range(2):
-                send[c, q, :, :, 128 * half : 128 * half + 128] = spread[c, q, half].reshape(4, RB, 128).astype(BF)
+                send[first + q, :, :, 128 * half : 128 * half + 128] = (
+                    spread[first + q, half].reshape(4, RB, 128).astype(BF)
+                )
+
+    def sums(c):
+        if c < STAGED:
+            with scope("x_wait"):
+                x_copy(c).wait_recv()
+            lay(c, c * half_q, half_q, lambda p, k, q: kept[c, p, k, q] + x_take[c, p, k, q].astype(F32))
+        else:
+            for p in range(PC):
+                core_copy(c * PC + p).wait_recv()
+            lay(
+                c, STAGED * half_q + (c - STAGED) * NQ, NQ,
+                lambda p, k, q: own[c * PC + p, k * NQ + q] + take[c * PC + p, k * NQ + q].astype(F32),
+            )
+
+    def place_of(c, px, pz):
+        return (c * half_q if c < STAGED else STAGED * half_q + (c - STAGED) * NQ + px * half_q) + pz // 4
+
+    def slot_of(c):
+        return c * NZ + z if c < STAGED else STAGED * NZ + (c - STAGED) * NX * NZ + chip
 
     def give_out(c, later):
-        for dz in owner_offsets():
-            pz = (z + dz + NZ) % NZ
+        for dx, dz in owner_offsets(1 if c < STAGED else NX):
+            px, pz = (xh + dx) % NX, (z + dz + NZ) % NZ
             known = rank_of(pz // CUBE) <= rank
 
             @pl.when(jnp.logical_not(known) if later else known)
             def _():
                 pltpu.make_async_remote_copy(
-                    src_ref=send.at[c, pz // 4, pz % 4], dst_ref=recv.at[c, z],
-                    send_sem=rs_send, recv_sem=rs_recv.at[c],
-                    device_id=(param_at(0, dz), qj), device_id_type=MESH,
+                    src_ref=send.at[place_of(c, px, pz), pz % 4], dst_ref=recv.at[slot_of(c)],
+                    send_sem=rs_send, recv_sem=rs_recv,
+                    device_id=(param_at(dx, dz), qj), device_id_type=MESH,
                 ).start()
         if not later:
-            recv[c, z] = jnp.zeros((RB, NG), BF)
-
-    for c in range(NC):
+            recv[slot_of(c)] = jnp.zeros((RB, NG), BF)
+
+    def products(c):
         with scope(f"ag_wait{c}"):
-            pltpu.make_async_copy(ag_all(c), ag_all(c), ag_recv.at[c]).wait()
+            ag_wait(c)
         with scope(f"products{c}"):
             for p in range(PC):
                 product(c * PC + p)
-        if c > 0:
-            with scope(f"across{c - 1}"):
-                across(c - 1)
-    with scope(f"across{NC - 1}"):
-        across(NC - 1)
-    for c in range(NC):
+
+    def leave(c):
         with scope(f"sums{c}"):
             sums(c)
         with scope(f"rs_start{c}"):
             give_out(c, False)
+
+    for c in range(NC):
+        products(c)
+        if 2 <= c < STAGED + 2:
+            with scope(f"across{c - 2}"):
+                across(c - 2)
+        elif c - 2 >= STAGED:
+            leave(c - 2)
+    for c in range(max(NC - 2, 0), NC):
+        if c < STAGED:
+            with scope(f"across{c}"):
+                across(c)
+        else:
+            leave(c)
+    for c in range(STAGED):
+        leave(c)
 
     @pl.when(rank < NZ // CUBE - 1)
     def _():
@@ -296,26 +367,35 @@
             for c in range(NC):
                 give_out(c, True)
 
-    mine = z // 4
-    onehot = (lax.broadcasted_iota(jnp.int32, (128, NG), 0) % GROUPS == group_v[...]).astype(F32)
+    onehot = (lax.broadcasted_iota(jnp.int32, (128, NG), 0) % GROUPS == group_v[...]).astype(F32).astype(BF)
+    with scope("rs_wait"):
+        whole = recv.at[pl.ds(0, ARRIVALS)]
+        pltpu.make_async_copy(whole, whole, rs_recv).wait()
     for c in range(NC):
-        with scope(f"rs_wait{c}"):
-            whole = recv.at[c, pl.ds(0, NZ - 1)]
-            pltpu.make_async_copy(whole, whole, rs_recv.at[c]).wait()
         with scope(f"final{c}"):
             at = pl.multiple_of((z % 4) * RB, RB)
-            here = jnp.concatenate([spread[c, mine, half, pl.ds(at, RB), :] for half in range(2)], axis=1)
-            total = here + jnp.sum(recv[c].astype(F32), axis=0)
+            mine = place_of(c, xh, z)
+            here = jnp.concatenate([spread[mine, half, pl.ds(at, RB), :] for half in range(2)], axis=1)
+            if c < STAGED:
+                slots = slice(c * NZ, (c + 1) * NZ)
+            else:
+                slots = slice(STAGED * NZ + (c - STAGED) * NX * NZ, STAGED * NZ + (c - STAGED + 1) * NX * NZ)
+            total = here + jnp.sum(recv[slots].astype(F32), axis=0)
             for f2 in range(2):
                 for k in range(2):
                     for p in range(PC):
                         row = (f2 * 2 + k) * PC + p
                         acc_out[k, (c * PC + p) * 2 + f2 : (c * PC + p) * 2 + f2 + 1, :] = total[row : row + 1]
     with scope("segment"):
-        grouped = lax.dot_general(
-            acc_out[...].reshape(16, NG), onehot, (((1,), (1,)), ((), ())),
-            precision=lax.Precision.HIGHEST, preferred_element_type=F32,
+        sums_all = acc_out[...].reshape(16, NG)
+        top = sums_all.astype(BF)
+        rest = sums_all - top.astype(F32)
+        middle = rest.astype(BF)
+        low = (rest - middle.astype(F32)).astype(BF)
+        terms = lax.dot_general(
+            jnp.concatenate([top, middle, low], axis=0), onehot, (((1,), (1,)), ((), ())), preferred_element_type=F32
         )
+        grouped = terms[:16] + terms[16:32] + terms[32:]
         segs[qj] = jnp.sum(jnp.where(diagonal((2, NF, 128)), grouped.reshape(2, NF, 128), 0.0), axis=1)
         seg = [
             pltpu.make_async_remote_copy(
@@ -327,7 +407,7 @@
         for copy in seg:
             copy.start()
     with scope("send_waits"):
-        whole = recv.at[:, pl.ds(0, NZ - 1)]
+        whole = recv.at[pl.ds(0, ARRIVALS)]
         pltpu.make_async_copy(whole, whole, rs_send).wait()
         sent = spectra.at[pl.ds(0, NQ - 1)]
         pltpu.make_async_copy(sent, sent, ag_send).wait()
@@ -365,12 +445,12 @@
             pltpu.VMEM((4, 2 * NQ, 8, NG), BF),
             pltpu.VMEM((4, 2 * NQ, 8, NG), BF),
             pltpu.VMEM((4, 2 * NQ, 8, NG), F32),
-            pltpu.VMEM((NC, PC, 2, NQ // NX, 8, NG), BF),
-            pltpu.VMEM((NC, PC, 2, NQ // NX, 8, NG), BF),
-            pltpu.VMEM((NC, PC, 2, NQ // NX, 8, NG), F32),
-            pltpu.VMEM((NC, NQ // NX, 2, 8 * 2 * PC, 128), F32),
-            pltpu.VMEM((NC, NQ // NX, 4, RB, NG), BF),
-            pltpu.VMEM((NC, NZ, RB, NG), BF),
+            pltpu.VMEM((STAGED, PC, 2, NQ // NX, 8, NG), BF),
+            pltpu.VMEM((STAGED, PC, 2, NQ // NX, 8, NG), BF),
+            pltpu.VMEM((STAGED, PC, 2, NQ // NX, 8, NG), F32),
+            pltpu.VMEM((SLOTS // 4, 2, 8 * 2 * PC, 128), F32),
+            pltpu.VMEM((SLOTS // 4, 4, RB, NG), BF),
+            pltpu.VMEM((SLOTS, RB, NG), BF),
             pltpu.VMEM((NQ, 2, 128), F32),
             pltpu.VMEM((1, NG), jnp.int32),
             dma((len(STEPS),)),
@@ -378,14 +458,16 @@
             dma,
             dma,
             dma((NC,)),
+            dma((NC,)),
             dma,
             dma((4,)),
             dma,
             dma((NC,)),
             dma,
-            dma((NC,)),
-            dma,
-            dma,
+            dma,
+            dma,
+            dma,
+            pltpu.SemaphoreType.REGULAR,
             pltpu.SemaphoreType.REGULAR,
             pltpu.SemaphoreType.REGULAR,
         ],

time: 42.9 us -> 41.5 us (0.967)
  Pallas kernels: 41.5 us -> 40.1 us
    pallas_call x1, Pallas kernels: 40.8 us -> 39.4 us  [local(): pl.pallas_call(kernel, out_shape=(pltpu.VMEM((2, NF, NG), F32), pltpu.VME...]
where the time goes in v3:
time: 41.5 us; the launch traced here: 41.3 us
  Pallas kernels  40.1 us (97%)
  between operations  1.28 us (3%)
    pallas_call x1, Pallas kernels, local(): pl.pallas_call(kernel, out_shape=(pltpu.VMEM((2, NF, NG), F32), pltpu.VME...  39.4 us

profile of v3, /device:TPU:2, one launch (start us, length us, event | category | flops | bytes accessed | tf_op | source)
XLA Modules:
  0.0 41.3 jit_solution(6290081556486648686)
XLA Ops:
  1.3 39.4 %shard_map.59 = (f32[2,8,256]{2,1,0:T(8,128)S(1)}, f32[2,128]{1,0:T(2,128)S(1)}) custom-call(bf16[420,8,320]{2,1,0:T(8,128)(2,1)} %bitcast.2, bf16[8,320,2,256]{3,2,1,0:T(2,128)(2,1)} %w_hbm.1, s32[1]{0:T(128)S(6)} %copy.6.first_ref, s32[1,256]{1,0:T(1,128)} %bitcast.3), custom_call_target="tpu_custom_call" | custom-call | tf_op jit(solution)/shard_map/pallas_call | solution.py:432
  40.7 0.7 %shard_map.60 = (f32[1,2,8,256]{3,2,1,0:T(8,128)}, f32[1,2,8,16]{3,2,1,0:T(8,128)}) custom-call(f32[2,8,256]{2,1,0:T(8,128)S(1)} %get-tuple-element.4.acc_ref, f32[2,128]{1,0:T(2,128)S(1)} %get-tuple-element.5.seg_ref), custom_call_target="tpu_custom_call" | custom-call | tf_op jit(solution)/shard_map/pallas_call | solution.py:476
